TPU v7x, 32 devices: a whole 2x2x4 slice. The times are simulated.
32 devices in a mesh: row: 4 (over y, core), col: 8 (over z, x).
Axes of the slice: x: 2, y: 2, z: 4, core: 2. Of those that a mesh axis runs over, the one named last changes fastest.
Arguments:
- rhs: bfloat16 [6144, 6144], P('row', 'col'), may hold values from -6 to 6
- basis_left: bfloat16 [6144, 6144], P('col', 'row'), may hold values from -1 to 1, as said below
- basis_right: bfloat16 [6144, 6144], P('row', 'col'), may hold values from -1 to 1, as said below
- eig_left: float32 [6144], P('row'), may hold values from 0.1 to 4
- eig_right: float32 [6144], P('col'), may hold values from 0.1 to 4
Outputs:
- solution: bfloat16 [6144, 6144], P('col', 'row')
Inputs may be any that keep to these rules, and one draw needn't show every extreme that they name: `basis_left`: an orthogonal matrix drawn uniformly, rounded to bfloat16. `basis_right`: an orthogonal matrix drawn uniformly, rounded to bfloat16.
All inputs are finite; a program needn't handle non-finite values.
Results may differ from a plain program's by a relative error of at most 0.0085.
Values may be sent and summed in bfloat16 or wider, within the bound.
A program may use at most 128 MiB of HBM per device.

v0:
```python
import jax
import jax.numpy as jnp
from jax import lax
from jax.sharding import PartitionSpec as P


def body(rhs, basis_left, basis_right, eig_left, eig_right):
    c_strip = lax.all_gather(rhs, "row", axis=0, tiled=True)
    left_all = lax.all_gather(basis_left, "col", axis=0, tiled=True)
    first = lax.dot_general(
        left_all, c_strip, (((0,), (0,)), ((), ())), preferred_element_type=jnp.float32
    )
    projected = first.astype(jnp.bfloat16)
    right_strip = lax.all_gather(basis_right, "row", axis=0, tiled=True)
    chosen = right_strip
    second = jnp.dot(
        lax.all_gather(projected, "col", axis=1, tiled=True),
        chosen,
        preferred_element_type=jnp.float32,
    )
    scaled = (second / (eig_left[:, None] + eig_right[None, :])).astype(jnp.bfloat16)
    chosen = left_all
    half = lax.psum_scatter(
        jnp.dot(chosen, scaled, preferred_element_type=jnp.float32),
        "row",
        scatter_dimension=0,
        tiled=True,
    ).astype(jnp.bfloat16)
    half_all = lax.all_gather(half, "row", axis=0, tiled=True)
    chosen = half_all
    return lax.psum_scatter(
        lax.dot_general(
            chosen, basis_right, (((1,), (1,)), ((), ())), preferred_element_type=jnp.float32
        ),
        "col",
        scatter_dimension=0,
        tiled=True,
    ).astype(jnp.bfloat16)


def solution(mesh):
    in_specs = (P("row", "col"), P("col", "row"), P("row", "col"), P("row"), P("col"))
    out_specs = P("col", "row")
    return jax.shard_map(body, mesh=mesh, in_specs=in_specs, out_specs=out_specs, check_vma=False)
```

profile of v0, /device:TPU:0, one launch (start us, length us, event | category | flops | bytes accessed | tf_op | source)
XLA Modules:
  0.0 1751.5 jit_solution(14869084896472922109)
XLA Ops:
  6.5 0.0 all-gather.8.cloned.1.call-start
  6.5 0.7 all-gather.8.cloned.1.call-update
  7.3 0.0 all-gather.6.cloned.1.call-start
  7.3 0.7 all-gather.6.cloned.1.call-update
  8.0 0.0 all-gather.12.cloned.1.call-start
  8.1 0.7 all-gather.12.cloned.1.call-update
  8.7 0.0 copy-start.1
  8.8 0.0 copy-start.2
  8.8 0.0 all-gather.10.cloned.1.call-start
  8.8 67.1 %all-gather.8.cloned.1.call-done = bf16[6144,768]{1,0:T(8,128)(2,1)} async-done(((bf16[1536,768]{1,0:T(8,128)(2,1)}), bf16[6144,768]{1,0:T(8,128)(2,1)}) %all-gather.8.cloned.1.call-update) | async-done | bytes 9437200 | tf_op jit(solution)/shard_map/all_gather | solution.py:8
  75.9 364.0 %all-gather.6.cloned.1.call-done = bf16[6144,1536]{1,0:T(8,128)(2,1)} async-done(((bf16[768,1536]{1,0:T(8,128)(2,1)}), bf16[6144,1536]{1,0:T(8,128)(2,1)}) %all-gather.6.cloned.1.call-update) | async-done | bytes 18874384 | tf_op jit(solution)/shard_map/all_gather | solution.py:9
  439.8 21.5 %convolution_convert_fusion = bf16[1536,768]{1,0:T(8,128)(2,1)} fusion(bf16[6144,1536]{1,0:T(8,128)(2,1)} %all-gather.6.cloned.1.call-done, bf16[6144,768]{1,0:T(8,128)(2,1)} %all-gather.8.cloned.1.call-done), kind=kOutput, calls=%fused_computation.2 | convolution fusion | flops 14496694272 | bytes 30670848 | tf_op jit(solution)/shard_map/dot_general | solution.py:10
  461.3 0.0 all-gather.10.cloned.1.call-update
  461.3 0.2 reduce-scatter.3.cloned.1.call-start
  461.5 44.1 %all-gather.12.cloned.1.call-done = bf16[6144,768]{1,0:T(8,128)(2,1)} async-done(((bf16[1536,768]{1,0:T(8,128)(2,1)}), bf16[6144,768]{1,0:T(8,128)(2,1)}) %all-gather.12.cloned.1.call-update) | async-done | bytes 9437200 | tf_op jit(solution)/shard_map/all_gather | solution.py:14
  505.6 363.8 %all-gather.10.cloned.1.call-done = bf16[1536,6144]{1,0:T(8,128)(2,1)} async-done(((bf16[1536,768]{1,0:T(8,128)(2,1)}), bf16[1536,6144]{1,0:T(8,128)(2,1)}) %all-gather.10.cloned.1.call-update) | async-done | bytes 18874384 | tf_op jit(solution)/shard_map/all_gather | solution.py:17
  869.4 0.0 copy-done.1
  869.4 0.0 copy-done.2
  869.4 20.6 %divide_convert_fusion = bf16[1536,768]{1,0:T(8,128)(2,1)S(1)} fusion(bf16[1536,6144]{1,0:T(8,128)(2,1)} %all-gather.10.cloned.1.call-done, bf16[6144,768]{1,0:T(8,128)(2,1)} %all-gather.12.cloned.1.call-done, f32[768]{0:T(1024)S(1)} %copy-done.2, f32[1536]{0:T(1024)S(1)} %copy-done.1), kind=kOutput, calls=%fused_computation.1 | convolution fusion | flops 14499053568 | bytes 30680064 | tf_op jit(solution)/shard_map/dot_general | solution.py:16
  890.1 20.7 %convolution_bitcast_fusion = f32[6144,768]{0,1:T(8,128)} fusion(bf16[1536,768]{1,0:T(8,128)(2,1)S(1)} %divide_convert_fusion, bf16[6144,1536]{1,0:T(8,128)(2,1)} %all-gather.6.cloned.1.call-done), kind=kOutput, calls=%fused_computation | convolution fusion | flops 14495514624 | bytes 40108032 | tf_op jit(solution)/shard_map/dot_general | solution.py:24
  910.8 0.0 reduce-scatter.3.cloned.1.call-update
  910.8 0.0 copy-start
  910.8 0.0 all-gather.14.cloned.1.call-start
  910.9 137.8 %reduce-scatter.3.cloned.1.call-done = f32[1536,768]{0,1:T(8,128)} async-done(((f32[6144,768]{0,1:T(8,128)}), f32[1536,768]{0,1:T(8,128)}) %reduce-scatter.3.cloned.1.call-update) | async-done | bytes 4718608 | tf_op jit(solution)/shard_map/reduce_scatter | solution.py:23
  1048.7 4.0 convert_element_type.14
  1052.7 0.0 all-gather.14.cloned.1.call-update
  1052.7 0.3 reduce-scatter.5.cloned.1.call-start
  1053.0 64.1 %all-gather.14.cloned.1.call-done = bf16[6144,768]{0,1:T(8,128)(2,1)} async-done(((bf16[1536,768]{0,1:T(8,128)(2,1)}), bf16[6144,768]{0,1:T(8,128)(2,1)}) %all-gather.14.cloned.1.call-update) | async-done | bytes 9437200 | tf_op jit(solution)/shard_map/all_gather | solution.py:29
  1117.1 0.0 copy-done
  1117.1 22.7 %fusion = f32[6144,1536]{1,0:T(8,128)} fusion(bf16[6144,768]{0,1:T(8,128)(2,1)} %all-gather.14.cloned.1.call-done, bf16[1536,768]{1,0:T(8,128)(2,1)S(1)} %copy-done), kind=kOutput, calls=%fused_computation.3 | convolution fusion | flops 14495514624 | bytes 49545216 | tf_op jit(solution)/shard_map/dot_general | solution.py:32
  1139.8 0.0 reduce-scatter.5.cloned.1.call-update
  1139.8 600.8 %reduce-scatter.5.cloned.1.call-done = f32[768,1536]{1,0:T(8,128)} async-done(((f32[6144,1536]{1,0:T(8,128)}), f32[768,1536]{1,0:T(8,128)}) %reduce-scatter.5.cloned.1.call-update) | async-done | bytes 4718608 | tf_op jit(solution)/shard_map/reduce_scatter | solution.py:31
  1740.6 4.0 convert_element_type.15
Async XLA Ops:
  6.5 69.3 %all-gather.8.cloned.1.call-start = ((), (), s32[]{:S(2)}) async-start(), calls=%async_computation.3 | async-start | bytes 11796480 | tf_op jit(solution)/shard_map/all_gather | solution.py:8
  7.3 432.6 %all-gather.6.cloned.1.call-start = ((), (), s32[]{:S(2)}) async-start(), calls=%async_computation.2 | async-start | bytes 21233664 | tf_op jit(solution)/shard_map/all_gather | solution.py:9
  8.0 497.6 %all-gather.12.cloned.1.call-start = ((), (), s32[]{:S(2)}) async-start(), calls=%async_computation.5 | async-start | bytes 11796480 | tf_op jit(solution)/shard_map/all_gather | solution.py:14
  8.7 860.7 %copy-start.1 = (f32[1536]{0:T(1024)S(1)}, f32[1536]{0:T(1024)}, u32[]{:S(2)}) copy-start(f32[1536]{0:T(1024)} %param.8) | copy-start | bytes 18436
  8.8 860.7 %copy-start.2 = (f32[768]{0:T(1024)S(1)}, f32[768]{0:T(1024)}, u32[]{:S(2)}) copy-start(f32[768]{0:T(1024)} %param.9) | copy-start | bytes 9220
  8.8 860.7 %all-gather.10.cloned.1.call-start = ((), (), s32[]{:S(2)}) async-start(), calls=%async_computation.4 | async-start | bytes 21233664 | tf_op jit(solution)/shard_map/all_gather | solution.py:17
  461.3 587.4 %reduce-scatter.3.cloned.1.call-start = ((), (), s32[]{:S(2)}) async-start(), calls=%async_computation.6 | async-start | bytes 23592960 | tf_op jit(solution)/shard_map/reduce_scatter | solution.py:23
  910.8 206.3 %copy-start = (bf16[1536,768]{1,0:T(8,128)(2,1)S(1)}, bf16[1536,768]{1,0:T(8,128)(2,1)}, u32[]{:S(2)}) copy-start(bf16[1536,768]{1,0:T(8,128)(2,1)} %param.7) | copy-start | bytes 7077892
  910.8 206.3 %all-gather.14.cloned.1.call-start = ((), (), s32[]{:S(2)}) async-start(), calls=%async_computation.7 | async-start | bytes 11796480 | tf_op jit(solution)/shard_map/all_gather | solution.py:29
  1052.7 687.9 %reduce-scatter.5.cloned.1.call-start = ((), (), s32[]{:S(2)}) async-start(), calls=%async_computation.8 | async-start | bytes 42467328 | tf_op jit(solution)/shard_map/reduce_scatter | solution.py:31
Sparse Core Ops, SparseCore 0:
  8.9 66.9 all-gather.7
  77.4 362.3 all-gather.5
  441.4 64.1 all-gather.11
  507.0 362.3 all-gather.9
  910.9 137.7 reduce-scatter.2
  1052.8 64.2 all-gather.13
  1139.9 600.6 reduce-scatter.4
where the time goes:
time: 1750 us
  waiting for transfers between devices  1640 us (94%)
  matrix products  85.5 us (5%)
    reduce_scatter x1, waiting for transfers between devices, body(): lax.psum_scatter(lax.dot_general(chosen, basis_right, (((1,), (1,)), ((),...  601 us
    all_gather x1, waiting for transfers between devices, body(): left_all = lax.all_gather(basis_left, 'col', axis=0, tiled=True)  364 us
    all_gather x1, waiting for transfers between devices, body(): lax.all_gather(projected, 'col', axis=1, tiled=True)  364 us
    reduce_scatter x1, waiting for transfers between devices, body(): lax.psum_scatter(jnp.dot(chosen, scaled, preferred_element_type=jnp.float...  138 us
    all_gather x1, waiting for transfers between devices, body(): c_strip = lax.all_gather(rhs, 'row', axis=0, tiled=True)  67.1 us
    all_gather x1, waiting for transfers between devices, body(): half_all = lax.all_gather(half, 'row', axis=0, tiled=True)  64.1 us
    all_gather x1, waiting for transfers between devices, body(): right_strip = lax.all_gather(basis_right, 'row', axis=0, tiled=True)  44.1 us
  transfers between devices with their start and end apart: 7, of which 7 were waited for; matrix products, arithmetic and copies ran while one was open for 1% of the time, Pallas kernels for 0%

commit v1 on v0

--- a/solution.py
+++ b/solution.py
@@ -14,7 +14,7 @@
     right_strip = lax.all_gather(basis_right, "row", axis=0, tiled=True)
     chosen = right_strip
     second = jnp.dot(
-        lax.all_gather(projected, "col", axis=1, tiled=True),
+        jnp.concatenate(lax.all_gather(projected, "col"), axis=1),
         chosen,
         preferred_element_type=jnp.float32,
     )

time: 1750 us -> 1770 us (1.011)
  local copies, waits for them, and re-layouts: 0.01 us -> 24 us
    all_gather x0 -> x1, local copies, waits for them, and re-layouts: none -> 24 us  [body(): lax.all_gather(projected, 'col')]
where the time goes in v1:
time: 1770 us
  waiting for transfers between devices  1640 us (93%)
  matrix products  85.7 us (5%)
  local copies, waits for them, and re-layouts  24 us (1%)
    reduce_scatter x1, waiting for transfers between devices, body(): lax.psum_scatter(lax.dot_general(chosen, basis_right, (((1,), (1,)), ((),...  601 us
    all_gather x1, waiting for transfers between devices, body(): left_all = lax.all_gather(basis_left, 'col', axis=0, tiled=True)  364 us
    all_gather x1, waiting for transfers between devices, body(): lax.all_gather(projected, 'col')  362 us
    reduce_scatter x1, waiting for transfers between devices, body(): lax.psum_scatter(jnp.dot(chosen, scaled, preferred_element_type=jnp.float...  138 us
    all_gather x1, waiting for transfers between devices, body(): c_strip = lax.all_gather(rhs, 'row', axis=0, tiled=True)  67.8 us
    all_gather x1, waiting for transfers between devices, body(): half_all = lax.all_gather(half, 'row', axis=0, tiled=True)  64.1 us
    all_gather x1, waiting for transfers between devices, body(): right_strip = lax.all_gather(basis_right, 'row', axis=0, tiled=True)  41.6 us
  transfers between devices with their start and end apart: 7, of which 7 were waited for; matrix products, arithmetic and copies ran while one was open for 1% of the time, Pallas kernels for 0%

profile of v1, /device:TPU:0, one launch (start us, length us, event | category | flops | bytes accessed | tf_op | source)
XLA Modules:
  0.0 1772.0 jit_solution(18214648041656031868)
XLA Ops:
  6.5 0.0 all-gather.9.cloned.1.call-start
  6.5 0.7 all-gather.9.cloned.1.call-update
  7.3 0.0 all-gather.7.cloned.1.call-start
  7.3 0.7 all-gather.7.cloned.1.call-update
  8.0 0.0 all-gather.15.cloned.1.call-start
  8.1 67.8 %all-gather.9.cloned.1.call-done = bf16[6144,768]{1,0:T(8,128)(2,1)} async-done(((bf16[1536,768]{1,0:T(8,128)(2,1)}), bf16[6144,768]{1,0:T(8,128)(2,1)}) %all-gather.9.cloned.1.call-update) | async-done | bytes 9437200 | tf_op jit(solution)/shard_map/all_gather | solution.py:8
  75.9 364.0 %all-gather.7.cloned.1.call-done = bf16[6144,1536]{1,0:T(8,128)(2,1)} async-done(((bf16[768,1536]{1,0:T(8,128)(2,1)}), bf16[6144,1536]{1,0:T(8,128)(2,1)}) %all-gather.7.cloned.1.call-update) | async-done | bytes 18874384 | tf_op jit(solution)/shard_map/all_gather | solution.py:9
  439.8 21.5 %convolution_convert_fusion = bf16[1536,768]{1,0:T(8,128)(2,1)} fusion(bf16[6144,1536]{1,0:T(8,128)(2,1)} %all-gather.7.cloned.1.call-done, bf16[6144,768]{1,0:T(8,128)(2,1)} %all-gather.9.cloned.1.call-done), kind=kOutput, calls=%fused_computation.2 | convolution fusion | flops 14496694272 | bytes 30670848 | tf_op jit(solution)/shard_map/dot_general | solution.py:10
  461.3 0.0 all-gather.15.cloned.1.call-update
  461.3 0.0 all-gather.11.cloned.1.call-start
  461.4 0.5 all-gather.11.cloned.1.call-update
  461.9 0.2 reduce-scatter.3.cloned.1.call-start
  462.1 361.7 %all-gather.15.cloned.1.call-done = bf16[12288,768]{1,0:T(8,128)(2,1)} async-done(((bf16[1536,768]{1,0:T(8,128)(2,1)}), bf16[12288,768]{1,0:T(8,128)(2,1)}) %all-gather.15.cloned.1.call-update) | async-done | bytes 18874384 | tf_op jit(solution)/shard_map/all_gather | solution.py:17
  823.8 0.0 copy-start.1
  823.8 0.0 copy-start.2
  823.8 24.0 %copy.6 = bf16[8,1536,768]{1,2,0:T(8,128)(2,1)} copy(bf16[8,1536,768]{2,1,0:T(8,128)(2,1)} %bitcast.14) | data formatting | bytes 37748736 | tf_op jit(solution)/shard_map/all_gather | solution.py:17
  847.8 41.6 %all-gather.11.cloned.1.call-done = bf16[6144,768]{1,0:T(8,128)(2,1)} async-done(((bf16[1536,768]{1,0:T(8,128)(2,1)}), bf16[6144,768]{1,0:T(8,128)(2,1)}) %all-gather.11.cloned.1.call-update) | async-done | bytes 9437200 | tf_op jit(solution)/shard_map/all_gather | solution.py:14
  889.5 0.0 copy-done.1
  889.5 0.0 copy-done.2
  889.5 20.9 %divide_convert_fusion = bf16[1536,768]{1,0:T(8,128)(2,1)S(1)} fusion(bf16[1536,6144]{0,1:T(8,128)(2,1)} %bitcast.15, bf16[6144,768]{1,0:T(8,128)(2,1)} %all-gather.11.cloned.1.call-done, f32[768]{0:T(1024)S(1)} %copy-done.2, f32[1536]{0:T(1024)S(1)} %copy-done.1), kind=kOutput, calls=%fused_computation.1 | convolution fusion | flops 14499053568 | bytes 30680064 | tf_op jit(solution)/shard_map/dot_general | solution.py:16
  910.3 20.7 %convolution_bitcast_fusion = f32[6144,768]{0,1:T(8,128)} fusion(bf16[1536,768]{1,0:T(8,128)(2,1)S(1)} %divide_convert_fusion, bf16[6144,1536]{1,0:T(8,128)(2,1)} %all-gather.7.cloned.1.call-done), kind=kOutput, calls=%fused_computation | convolution fusion | flops 14495514624 | bytes 40108032 | tf_op jit(solution)/shard_map/dot_general | solution.py:24
  931.1 0.0 reduce-scatter.3.cloned.1.call-update
  931.1 0.0 copy-start
  931.1 0.0 all-gather.13.cloned.1.call-start
  931.1 137.8 %reduce-scatter.3.cloned.1.call-done = f32[1536,768]{0,1:T(8,128)} async-done(((f32[6144,768]{0,1:T(8,128)}), f32[1536,768]{0,1:T(8,128)}) %reduce-scatter.3.cloned.1.call-update) | async-done | bytes 4718608 | tf_op jit(solution)/shard_map/reduce_scatter | solution.py:23
  1069.0 4.0 convert_element_type.14
  1073.0 0.0 all-gather.13.cloned.1.call-update
  1073.0 0.3 reduce-scatter.5.cloned.1.call-start
  1073.3 64.1 %all-gather.13.cloned.1.call-done = bf16[6144,768]{0,1:T(8,128)(2,1)} async-done(((bf16[1536,768]{0,1:T(8,128)(2,1)}), bf16[6144,768]{0,1:T(8,128)(2,1)}) %all-gather.13.cloned.1.call-update) | async-done | bytes 9437200 | tf_op jit(solution)/shard_map/all_gather | solution.py:29
  1137.4 0.0 copy-done
  1137.4 22.7 %fusion = f32[6144,1536]{1,0:T(8,128)} fusion(bf16[6144,768]{0,1:T(8,128)(2,1)} %all-gather.13.cloned.1.call-done, bf16[1536,768]{1,0:T(8,128)(2,1)S(1)} %copy-done), kind=kOutput, calls=%fused_computation.3 | convolution fusion | flops 14495514624 | bytes 49545216 | tf_op jit(solution)/shard_map/dot_general | solution.py:32
  1160.0 0.0 reduce-scatter.5.cloned.1.call-update
  1160.1 601.1 %reduce-scatter.5.cloned.1.call-done = f32[768,1536]{1,0:T(8,128)} async-done(((f32[6144,1536]{1,0:T(8,128)}), f32[768,1536]{1,0:T(8,128)}) %reduce-scatter.5.cloned.1.call-update) | async-done | bytes 4718608 | tf_op jit(solution)/shard_map/reduce_scatter | solution.py:31
  1761.2 4.0 convert_element_type.15
Async XLA Ops:
  6.5 69.3 %all-gather.9.cloned.1.call-start = ((), (), s32[]{:S(2)}) async-start(), calls=%async_computation.3 | async-start | bytes 11796480 | tf_op jit(solution)/shard_map/all_gather | solution.py:8
  7.3 432.6 %all-gather.7.cloned.1.call-start = ((), (), s32[]{:S(2)}) async-start(), calls=%async_computation.2 | async-start | bytes 21233664 | tf_op jit(solution)/shard_map/all_gather | solution.py:9
  8.0 815.8 %all-gather.15.cloned.1.call-start = ((), (), s32[]{:S(2)}) async-start(), calls=%async_computation.8 | async-start | bytes 21233664 | tf_op jit(solution)/shard_map/all_gather | solution.py:17
  461.3 428.2 %all-gather.11.cloned.1.call-start = ((), (), s32[]{:S(2)}) async-start(), calls=%async_computation.4 | async-start | bytes 11796480 | tf_op jit(solution)/shard_map/all_gather | solution.py:14
  461.9 607.1 %reduce-scatter.3.cloned.1.call-start = ((), (), s32[]{:S(2)}) async-start(), calls=%async_computation.5 | async-start | bytes 23592960 | tf_op jit(solution)/shard_map/reduce_scatter | solution.py:23
  823.8 65.6 %copy-start.1 = (f32[1536]{0:T(1024)S(1)}, f32[1536]{0:T(1024)}, u32[]{:S(2)}) copy-start(f32[1536]{0:T(1024)} %param.8) | copy-start | bytes 18436
  823.8 65.6 %copy-start.2 = (f32[768]{0:T(1024)S(1)}, f32[768]{0:T(1024)}, u32[]{:S(2)}) copy-start(f32[768]{0:T(1024)} %param.9) | copy-start | bytes 9220
  931.1 206.3 %copy-start = (bf16[1536,768]{1,0:T(8,128)(2,1)S(1)}, bf16[1536,768]{1,0:T(8,128)(2,1)}, u32[]{:S(2)}) copy-start(bf16[1536,768]{1,0:T(8,128)(2,1)} %param.7) | copy-start | bytes 7077892
  931.1 206.3 %all-gather.13.cloned.1.call-start = ((), (), s32[]{:S(2)}) async-start(), calls=%async_computation.6 | async-start | bytes 11796480 | tf_op jit(solution)/shard_map/all_gather | solution.py:29
  1073.0 688.2 %reduce-scatter.5.cloned.1.call-start = ((), (), s32[]{:S(2)}) async-start(), calls=%async_computation.7 | async-start | bytes 42467328 | tf_op jit(solution)/shard_map/reduce_scatter | solution.py:31
Sparse Core Ops, SparseCore 0:
  8.9 66.9 all-gather.8
  77.4 362.3 all-gather.6
  461.4 362.3 all-gather.14
  825.2 64.1 all-gather.10
  931.2 137.7 reduce-scatter.2
  1073.1 64.1 all-gather.12
  1160.2 600.9 reduce-scatter.4
